TPU v7x, 128 devices: a whole 4x4x4 slice. The times are simulated.
128 devices in a mesh: ma: 32 (over y, z, core), pb: 4 (over x).
Axes of the slice: x: 4, y: 4, z: 4, core: 2. Of those that a mesh axis runs over, the one named last changes fastest.
Arguments:
- coefs: float32 [512, 1056, 64], P('ma', 'pb'), may hold values from -6 to 6
- legendre: float32 [512, 1056, 4, 256], P('ma', None, 'pb'), may hold values from -0.25 to 0.25
- quad_weight: float32 [4, 256], P('pb'), may hold values from 0.3 to 3
- pair_of_slot: int32 [512], replicated, may hold values from 0 to 511, each once
- tracers: float32 [12, 2, 1024, 2048], P(None, None, ('ma', 'pb')), may hold values from 0 to 2
- heat_rate: float32 [12, 2], replicated, may hold values from -1.75 to 1.75
Outputs:
- spec_tendency: float32 [512, 1056, 64], P('ma', 'pb')
- tracers_new: float32 [12, 2, 1024, 2048], P(None, None, ('ma', 'pb'))
Inputs may be any that keep to these rules, and one draw needn't show every extreme that they name: Each pair number appears once; slot s holds the orders pair_of_slot[s] and 1023 - pair_of_slot[s].
All inputs are finite; a program needn't handle non-finite values.
Results may differ from a plain program's by a relative error of at most 0.00007.
Values sent between devices are 32-bit elements; how exact they have to be, the bound alone decides.
No kernel may reach another device: no remote copies, remote signals or barrier semaphores. Data moves between devices by JAX's collectives and lax.ppermute only.
A program may use at most 128 MiB of HBM per device.

v0:
```python
import math
import jax
import jax.numpy as jnp
from jax import lax
from jax.sharding import PartitionSpec as P

M = 1024
NLAT = 1024
NLON = 2048
LAYER_TOTAL = 8
NF = 4
NTR = 12
TLEV = 2
PAIRS = 512
COURANT = 0.15
DRAG_COEFFICIENT = 0.2
MOISTURE_SOURCE = 0.3
RAINFALL_FACTOR = 0.2
HIGHEST = lax.Precision.HIGHEST


def extended(array, sides, width):
    edges = {}
    for axis, dim in sides:
        count, length = (lax.axis_size(axis), array.shape[dim])
        up = [(i, (i + 1) % count) for i in range(count - 1)]
        last = lax.slice_in_dim(array, length - width, length, axis=dim)
        initial = lax.slice_in_dim(array, 0, width, axis=dim)
        edges[dim] = (
            lax.ppermute(last, axis, up),
            lax.ppermute(initial, axis, [(b, a) for a, b in up]),
        )
    done = []
    for _, dim in sides:
        low, high = edges[dim]
        around = [(width, width) if d in done else (0, 0) for d in range(array.ndim)]
        array = jnp.concatenate([jnp.pad(low, around), array, jnp.pad(high, around)], axis=dim)
        done.append(dim)
    return array


def order_tables(pair_of_slot):
    orders = jnp.stack([pair_of_slot, M - 1 - pair_of_slot], axis=1)
    points = jnp.arange(NLON, dtype=jnp.int32)
    phases = orders[:, :, None] * points[None, None, :] % NLON
    angles = phases.astype(jnp.float32) * (2.0 * math.pi / NLON)
    factor = 1.0 / math.sqrt(NLON)
    fourier_table = jnp.stack([jnp.cos(angles) * factor, -jnp.sin(angles) * factor], axis=0)
    weights = jnp.where(orders == 0, 1.0, 2.0).astype(jnp.float32)
    return (fourier_table, weights)


def row_masks(pair_ids, row_count):
    row_ids = jnp.arange(row_count, dtype=jnp.int32)
    bounds = (M - pair_ids)[:, None]
    low_rows = row_ids[None, :] < bounds
    high_rows = (row_ids[None, :] >= bounds) & (row_ids[None, :] <= M)
    return (low_rows, high_rows)


def advect(padded, zonal_wind, southward, first_row):
    middle = padded[:, :, 1:-1, :]
    east_face = 0.5 * (zonal_wind + jnp.roll(zonal_wind, -1, axis=-1))
    flux_east = jnp.maximum(east_face, 0.0) * middle + jnp.minimum(east_face, 0.0) * jnp.roll(
        middle, -1, axis=-1
    )
    across = 0.5 * (southward[:, :-1, :] + southward[:, 1:, :])
    flux_south = (
        jnp.maximum(across, 0.0) * padded[:, :, :-1, :]
        + jnp.minimum(across, 0.0) * padded[:, :, 1:, :]
    )
    upper_row = first_row - 1 + jnp.arange(across.shape[1], dtype=jnp.int32)
    inside = (upper_row >= 0) & (upper_row <= NLAT - 2)
    flux_south = jnp.where(inside[None, None, :, None], flux_south, 0.0)
    change = (
        flux_east
        - jnp.roll(flux_east, 1, axis=-1)
        + (flux_south[:, :, 1:, :] - flux_south[:, :, :-1, :])
    )
    return -COURANT * change


def shards(coefs, legendre, quad_weight, pair_of_slot, tracers, heat_rate):
    slot_count = coefs.shape[0]
    row_block = coefs.shape[1]
    columns = coefs.shape[2]
    quarter = legendre.shape[3]
    legendre_rows = legendre.reshape(slot_count, legendre.shape[1], quarter)
    own_pairs = lax.dynamic_slice_in_dim(
        pair_of_slot, lax.axis_index("ma") * slot_count, slot_count, 0
    )
    row_piece = lax.all_gather(coefs, "pb", axis=1, tiled=True)
    row_count = row_piece.shape[1]
    low_rows, high_rows = row_masks(own_pairs, row_count)
    masked = jnp.concatenate(
        [
            jnp.where(low_rows[:, :, None], row_piece, 0.0),
            jnp.where(high_rows[:, :, None], row_piece, 0.0),
        ],
        axis=2,
    )
    table_rows = legendre_rows
    legendre_sum = jnp.einsum("srl,src->slc", table_rows, masked, precision=HIGHEST)
    bands = lax.all_to_all(legendre_sum, "ma", split_axis=1, concat_axis=0, tiled=True)
    band_rows = bands.shape[1]
    fourier_table, weights = order_tables(pair_of_slot)
    spectral = (
        bands.reshape(PAIRS, band_rows, 2, 2, NF * LAYER_TOTAL) * weights[:, None, :, None, None]
    )
    physical_space_field = jnp.einsum("sjhpc,pshi->jci", spectral, fourier_table, precision=HIGHEST)
    zonal_wind = jnp.transpose(physical_space_field[:, 0:TLEV, :], (1, 0, 2))
    southward = -jnp.transpose(
        physical_space_field[:, LAYER_TOTAL : LAYER_TOTAL + TLEV, :], (1, 0, 2)
    )
    first_row = lax.axis_index(("ma", "pb")) * band_rows
    stacked = jnp.concatenate([tracers, zonal_wind[None], southward[None]], axis=0)
    widened = extended(stacked, ((("ma", "pb"), 2),), 3)
    anchor = widened[:NTR]
    zonal_ext = widened[NTR]
    south_ext = widened[NTR + 1]
    first_section = anchor[:, :, 1:-1] + advect(
        anchor, zonal_ext[:, 1:-1], south_ext, first_row - 2
    )
    second = 0.75 * anchor[:, :, 2:-2] + 0.25 * (
        first_section[:, :, 1:-1]
        + advect(first_section, zonal_ext[:, 2:-2], south_ext[:, 1:-1], first_row - 1)
    )
    new_tracers = tracers / 3.0 + 2.0 / 3.0 * (
        second[:, :, 1:-1] + advect(second, zonal_ext[:, 3:-3], south_ext[:, 2:-2], first_row)
    )
    heating = jnp.einsum("kl,klji->jli", heat_rate, new_tracers, precision=HIGHEST)
    eastward_finished = physical_space_field[:, 0:LAYER_TOTAL]
    northward_velocity = physical_space_field[:, LAYER_TOTAL : 2 * LAYER_TOTAL]
    thermal_state = physical_space_field[:, 2 * LAYER_TOTAL : 3 * LAYER_TOTAL]
    vapour_mixing_share = physical_space_field[:, 3 * LAYER_TOTAL : 4 * LAYER_TOTAL]
    flow_speed_norm = jnp.sqrt(
        eastward_finished * eastward_finished + northward_velocity * northward_velocity + 1.0
    )
    warming_finished = jnp.pad(heating, ((0, 0), (0, LAYER_TOTAL - TLEV), (0, 0)))
    rate_of_change_field = jnp.concatenate(
        [
            -DRAG_COEFFICIENT * flow_speed_norm * eastward_finished,
            -DRAG_COEFFICIENT * flow_speed_norm * northward_velocity,
            warming_finished - MOISTURE_SOURCE * thermal_state * vapour_mixing_share,
            MOISTURE_SOURCE * thermal_state * vapour_mixing_share
            - RAINFALL_FACTOR * flow_speed_norm * vapour_mixing_share,
        ],
        axis=1,
    )
    fourier = jnp.einsum(
        "jci,pshi->sjhpc", rate_of_change_field, fourier_table, precision=HIGHEST
    ).reshape(PAIRS, band_rows, 2 * columns)
    by_orders = lax.all_to_all(fourier, "ma", split_axis=0, concat_axis=1, tiled=True)
    weighted = by_orders * quad_weight.reshape(quarter)[None, :, None]
    table_rows = legendre_rows
    row_sums = jnp.einsum("srl,slc->rsc", table_rows, weighted, precision=HIGHEST)
    low_rows, high_rows = row_masks(own_pairs, row_block * lax.axis_size("pb"))
    summed = lax.psum_scatter(
        jnp.where(low_rows.T[:, :, None], row_sums[:, :, :columns], 0.0)
        + jnp.where(high_rows.T[:, :, None], row_sums[:, :, columns:], 0.0),
        "pb",
        scatter_dimension=0,
        tiled=True,
    )
    return (jnp.transpose(summed, (1, 0, 2)), new_tracers)


def solution(mesh):
    in_specs = (
        P("ma", "pb", None),
        P("ma", None, "pb", None),
        P("pb", None),
        P(),
        P(None, None, ("ma", "pb"), None),
        P(),
    )
    out_specs = (P("ma", "pb", None), P(None, None, ("ma", "pb"), None))
    return jax.shard_map(shards, mesh=mesh, in_specs=in_specs, out_specs=out_specs, check_vma=False)
```

profile of v0, /device:TPU:1, one launch (start us, length us, event | category | flops | bytes accessed | tf_op | source)
XLA Modules:
  0.0 511.0 jit_solution(13479577784716797474)
XLA Ops:
  7.2 2.9 copy.83
  11.0 87.7 %all-gather.2.cloned.1.call-done = f32[16,1056,64]{2,1,0:T(8,128)} async-done(((f32[16,264,64]{2,1,0:T(8,128)}), f32[16,1056,64]{2,1,0:T(8,128)}) %all-gather.2.cloned.1.call-update) | async-done | bytes 4325392 | tf_op jit(solution)/shard_map/all_gather | solution.py:92
  98.6 10.0 %broadcast_select_fusion.1 = (f32[16,1056,64]{2,1,0:T(8,128)}, f32[16,1056,64]{2,1,0:T(8,128)}) fusion(f32[16,1056,64]{2,1,0:T(8,128)} %all-gather.2.cloned.1.call-done, pred[16,1056]{1,0:T(8,128)(4,1)S(1)} %get-tuple-element.42, pred[16,1056]{1,0:T(8,128)(4,1)S(1)} %get-tuple-element.43), kind=kLoop, calls=%fused_computation.30 | loop fusion | flops 2162688 | bytes 13009920 | tf_op jit(solution)/shard_map/jit(_where)/select_n | solution.py:97
  108.7 26.4 %fusion.60 = f32[16,256,128]{1,2,0:T(8,128)S(1)} fusion(f32[16,1056,1,256]{3,2,1,0:T(1,128)} %param.7, f32[16,1056,64]{2,1,0:T(8,128)} %get-tuple-element.19, f32[16,1056,64]{2,1,0:T(8,128)} %get-tuple-element.18), kind=kOutput, calls=%fused_computation.87 | convolution fusion | flops 6645940224 | bytes 28049408 | tf_op jit(solution)/shard_map/srl,src->slc/dot_general | solution.py:103
  135.1 2.0 copy.84
  137.1 7.9 %all-to-all-start = ((f32[16,256,128]{2,0,1:T(8,128)}), f32[16,256,128]{2,0,1:T(8,128)}, u32[]{:S(2)}, u32[]{:S(2)}) async-start(f32[16,256,128]{2,0,1:T(8,128)} %copy.84), calls=%async_computation | async-start | bytes 4194304 | tf_op jit(solution)/shard_map/all_to_all | solution.py:104
  145.2 2.3 copy.89
  147.6 37.4 %cosine_multiply_fusion = (f32[1,512,2,2048]{3,1,0,2:T(8,128)}, f32[1,512,2,2048]{3,1,0,2:T(8,128)}) fusion(s32[512,2]{0,1:T(2,128)S(1)} %pad_add_fusion), kind=kLoop, calls=%fused_computation.24 | loop fusion | flops 35651584 | bytes 16781312 | tf_op jit(solution)/shard_map/mul | solution.py:48
  184.9 3.8 copy.86
  188.7 10.0 %reshape.233 = f32[512,8,2,2,32]{4,3,2,1,0:T(2,128)} reshape(f32[32,16,8,128]{3,2,1,0:T(8,128)} %copy.86) | data formatting | bytes 4194304 | tf_op jit(solution)/shard_map/reshape | solution.py:108
  198.7 5.6 %broadcast_multiply_fusion = f32[512,8,2,2,32]{4,3,2,1,0:T(2,128)S(1)} fusion(f32[512,8,2,2,32]{4,3,2,1,0:T(2,128)} %reshape.233, f32[512,2]{1,0:T(8,128)S(1)} %copy.87), kind=kLoop, calls=%fused_computation.31 | loop fusion | flops 524288 | bytes 4198400 | tf_op jit(solution)/shard_map/mul | solution.py:108
  204.4 73.6 %fusion.33 = f32[8,32,2048]{2,1,0:T(8,128)S(1)} fusion(f32[512,8,2,2,32]{4,3,2,1,0:T(2,128)S(1)} %broadcast_multiply_fusion, f32[1,512,2,2048]{3,1,0,2:T(8,128)} %get-tuple-element.39, f32[1,512,2,2048]{3,1,0,2:T(8,128)} %get-tuple-element.38), kind=kOutput, calls=%fused_computation.53 | convolution fusion | flops 12889096192 | bytes 20971520 | tf_op jit(solution)/shard_map/sjhpc,pshi->jci/dot_general | solution.py:110
  279.8 3.1 collective-permute-start
  282.9 3.7 collective-permute-start.1
  287.7 14.4 %collective-permute-done = f32[14,2,3,2048]{3,0,2,1:T(8,128)S(1)} collective-permute-done((f32[14,2,3,2048]{3,0,2,1:T(8,128)}, f32[14,2,3,2048]{3,0,2,1:T(8,128)S(1)}, u32[]{:S(2)}, u32[]{:S(2)}) %collective-permute-start) | collective-permute-done | bytes 688160 | tf_op jit(solution)/shard_map/ppermute | solution.py:30
  303.6 1.8 pad_maximum_fusion.9
  309.0 1.6 pad_maximum_fusion
  311.5 2.4 fusion.30
  315.5 1.5 fusion.27
  320.4 1.6 fusion.40
  325.5 2.2 fusion.48
  327.7 1.6 fusion.80
  329.9 17.4 %fusion.57 = f32[512,8,2,2,32]{0,4,1,2,3:T(8,128)S(1)} fusion(f32[8,8,2048]{2,1,0:T(8,128)S(1)} %get-tuple-element.25, f32[8,8,2048]{2,1,0:T(8,128)S(1)} %get-tuple-element.26, f32[8,8,2048]{2,1,0:T(8,128)S(1)} %get-tuple-element.27, f32[8,8,2048]{2,1,0:T(8,128)S(1)} %get-tuple-element.24, f32[1,512,2,2048]{3,1,0,2:T(8,128)} %get-tuple-element.39, ...), kind=kOutput, calls=%fused_computation.86 | convolution fusion | flops 12890669056 | bytes 20971520 | tf_op jit(solution)/shard_map/jci,pshi->sjhpc/dot_general | solution.py:150
  347.2 1.6 copy.109
  348.8 2.9 copy.110
  351.8 8.7 %all-to-all-start.1 = ((f32[512,8,128]{2,1,0:T(8,128)}), f32[512,8,128]{2,1,0:T(8,128)}, u32[]{:S(2)}, u32[]{:S(2)}) async-start(f32[512,8,128]{2,1,0:T(8,128)} %copy.110), calls=%async_computation.1 | async-start | bytes 4194304 | tf_op jit(solution)/shard_map/all_to_all | solution.py:153
  360.6 28.2 %all-to-all-done.1 = f32[512,8,128]{2,1,0:T(8,128)} async-done(((f32[512,8,128]{2,1,0:T(8,128)}), f32[512,8,128]{2,1,0:T(8,128)}, u32[]{:S(2)}, u32[]{:S(2)}) %all-to-all-start.1) | async-done | bytes 2097184 | tf_op jit(solution)/shard_map/all_to_all | solution.py:153
  388.8 21.9 %fusion.20 = f32[1056,16,128]{2,0,1:T(8,128)S(1)} fusion(f32[16,1056,1,256]{3,2,1,0:T(1,128)} %param.7, f32[16,32,8,128]{3,2,0,1:T(8,128)} %bitcast.26, f32[256]{0:T(256)S(1)} %bitcast.86), kind=kOutput, calls=%fused_computation.28 | convolution fusion | flops 6644301824 | bytes 28050432 | tf_op jit(solution)/shard_map/srl,slc->rsc/dot_general | solution.py:156
  410.7 9.5 %fusion.8 = f32[1056,16,64]{2,0,1:T(8,128)} fusion(f32[1056,16,128]{2,0,1:T(8,128)S(1)} %fusion.20, pred[1056,16]{0,1:T(8,128)(4,1)S(1)} %get-tuple-element.41, pred[1056,16]{0,1:T(8,128)(4,1)S(1)} %get-tuple-element.40), kind=kLoop, calls=%fused_computation.13 | loop fusion | flops 3244032 | bytes 13009920 | tf_op jit(solution)/shard_map/add | solution.py:159
  420.2 2.1 copy.113
  422.3 78.4 %reduce-scatter.2.cloned.1.call-done = f32[264,16,64]{2,0,1:T(8,128)} async-done(((f32[1056,16,64]{2,0,1:T(8,128)}), f32[264,16,64]{2,0,1:T(8,128)}) %reduce-scatter.2.cloned.1.call-update) | async-done | bytes 1081360 | tf_op jit(solution)/shard_map/reduce_scatter | solution.py:158
  500.6 3.0 copy.112
  (99 shorter events, 18.5 us)
Async XLA Ops:
  7.2 320.5 %copy-start = (f32[12,2]{0,1:T(2,128)S(1)}, f32[12,2]{0,1:T(2,128)}, u32[]{:S(2)}) copy-start(f32[12,2]{0,1:T(2,128)} %param.11) | copy-start | bytes 292
  7.2 3.0 copy-start.9
  7.2 91.5 %all-gather.2.cloned.1.call-start = ((), (), s32[]{:S(2)}) async-start(), calls=%async_computation.3 | async-start | bytes 10813440 | tf_op jit(solution)/shard_map/all_gather | solution.py:92
  10.3 98.4 %copy-start.10 = (s32[16]{0:T(128)}, s32[16]{0:T(128)S(1)}, u32[]{:S(2)}) copy-start(s32[16]{0:T(128)S(1)} %dynamic-slice_subtract_fusion) | copy-start | bytes 196
  10.3 0.6 copy-start.7
  137.1 47.8 %all-to-all-start = ((f32[16,256,128]{2,0,1:T(8,128)}), f32[16,256,128]{2,0,1:T(8,128)}, u32[]{:S(2)}, u32[]{:S(2)}) async-start(f32[16,256,128]{2,0,1:T(8,128)} %copy.84), calls=%async_computation | async-start | bytes 4194304 | tf_op jit(solution)/shard_map/all_to_all | solution.py:104
  278.0 1.8 copy-start.2
  279.8 22.4 %collective-permute-start = (f32[14,2,3,2048]{3,0,2,1:T(8,128)}, f32[14,2,3,2048]{3,0,2,1:T(8,128)S(1)}, u32[]{:S(2)}, u32[]{:S(2)}) collective-permute-start(f32[14,2,3,2048]{3,0,2,1:T(8,128)} %get-tuple-element.22), channel_id=1, source_target_pairs={{0,1},{1,2},{2,3},{3,4},{4,5},{5,6},{6,7},{7,8},{8,9},{9,10},{10,1... | collective-permute-start | bytes 2064392 | tf_op jit(solution)/shard_map/ppermute | solution.py:30
  282.9 20.7 %collective-permute-start.1 = (f32[14,2,3,2048]{3,0,2,1:T(8,128)}, f32[14,2,3,2048]{3,0,2,1:T(8,128)}, u32[]{:S(2)}, u32[]{:S(2)}) collective-permute-start(f32[14,2,3,2048]{3,0,2,1:T(8,128)} %get-tuple-element.23), channel_id=1, source_target_pairs={{1,0},{2,1},{3,2},{4,3},{5,4},{6,5},{7,6},{8,7},{9,8},{10,9},{11,1... | collective-permute-start | bytes 2064392 | tf_op jit(solution)/shard_map/ppermute | solution.py:31
  318.5 1.2 copy-start.14
  322.0 0.9 copy-start.4
  322.0 1.0 copy-start.6
  322.1 1.0 copy-start.5
  323.2 0.9 copy-start.13
  324.1 1.4 copy-start.1
  324.7 5.1 %slice-start = ((s8[8388608]{0:T(1024)(128)(4,1)}), s8[4194304]{0:T(1024)(128)(4,1)S(1)}, s32[]{:S(2)}) async-start(s8[8388608]{0:T(1024)(128)(4,1)} %bitcast.77), calls=%async_computation.5 | async-start | bytes 8388608
  325.5 4.3 slice-start.1
  327.7 1.8 copy-start.3
  351.7 8.7 %copy-start.8 = (pred[1056]{0:T(1024)(128)(4,1)S(1)}, pred[1056]{0:T(1024)(128)(4,1)}, u32[]{:S(2)}) copy-start(pred[1056]{0:T(1024)(128)(4,1)} %copy-done.7) | copy-start | bytes 3172
  351.7 8.8 %copy-start.11 = (s32[16]{0:T(128)S(1)}, s32[16]{0:T(128)}, u32[]{:S(2)}) copy-start(s32[16]{0:T(128)} %copy-done.10) | copy-start | bytes 196
  351.8 37.1 %copy-start.12 = (f32[1,256]{1,0:T(1,128)S(1)}, f32[1,256]{1,0:T(1,128)}, u32[]{:S(2)}) copy-start(f32[1,256]{1,0:T(1,128)} %param.8) | copy-start | bytes 3076
  351.8 37.1 %all-to-all-start.1 = ((f32[512,8,128]{2,1,0:T(8,128)}), f32[512,8,128]{2,1,0:T(8,128)}, u32[]{:S(2)}, u32[]{:S(2)}) async-start(f32[512,8,128]{2,1,0:T(8,128)} %copy.110), calls=%async_computation.1 | async-start | bytes 4194304 | tf_op jit(solution)/shard_map/all_to_all | solution.py:153
  360.4 140.2 %reduce-scatter.2.cloned.1.call-start = ((), (), s32[]{:S(2)}) async-start(), calls=%async_computation.4 | async-start | bytes 10813440 | tf_op jit(solution)/shard_map/reduce_scatter | solution.py:158
Sparse Core Ops, SparseCore 0:
  10.3 88.2 all-gather.1
  420.3 80.2 reduce-scatter.1
where the time goes:
time: 520 us; the launch traced here: 511 us
  waiting for transfers between devices  210 us (40%)
  matrix products  141 us (27%)
  other arithmetic  81.8 us (16%)
  local copies, waits for them, and re-layouts  39.5 us (8%)
  starting transfers between devices  23.4 us (4%)
  between operations  15.1 us (3%)
    all_gather x1, waiting for transfers between devices, shards(): row_piece = lax.all_gather(coefs, 'pb', axis=1, tiled=True)  87.7 us
    reduce_scatter x1, waiting for transfers between devices, shards(): lax.psum_scatter(jnp.where(low_rows.T[:, :, None], row_sums[:, :, :column...  78.4 us
    dot_general x1, matrix products, shards(): jnp.einsum('sjhpc,pshi->jci', spectral, fourier_table, precision=HIGHEST)  73.6 us
    mul x1, other arithmetic, order_tables(): jnp.cos(angles) * factor  37.4 us
    all_to_all x1, waiting for transfers between devices, shards(): lax.all_to_all(fourier, 'ma', split_axis=0, concat_axis=1, tiled=True)  28.2 us
    dot_general x1, matrix products, shards(): jnp.einsum('srl,src->slc', table_rows, masked, precision=HIGHEST)  26.4 us
    dot_general x1, matrix products, shards(): jnp.einsum('srl,slc->rsc', table_rows, weighted, precision=HIGHEST)  21.9 us
    dot_general x1, matrix products, shards(): jnp.einsum('jci,pshi->sjhpc', rate_of_change_field, fourier_table, precis...  17.4 us
  transfers between devices with their start and end apart: 6, of which 5 were waited for; matrix products, arithmetic and copies ran while one was open for 8% of the time, Pallas kernels for 0%

commit v1 on v0

--- a/solution.py
+++ b/solution.py
@@ -89,7 +89,8 @@
     own_pairs = lax.dynamic_slice_in_dim(
         pair_of_slot, lax.axis_index("ma") * slot_count, slot_count, 0
     )
-    row_piece = lax.all_gather(coefs, "pb", axis=1, tiled=True)
+    parts = lax.all_gather(coefs, "pb")
+    row_piece = jnp.concatenate(parts, axis=1)
     row_count = row_piece.shape[1]
     low_rows, high_rows = row_masks(own_pairs, row_count)
     masked = jnp.concatenate(

time: 520 us -> 509 us (0.979)
  waiting for transfers between devices: 210 us -> 192 us
  local copies, waits for them, and re-layouts: 39.5 us -> 45.8 us
    all_gather x1, waiting for transfers between devices: 87.7 us -> 68.5 us  [shards(): parts = lax.all_gather(coefs, 'pb')]
    all_gather x0 -> x1, local copies, waits for them, and re-layouts: none -> 8.8 us  [shards(): parts = lax.all_gather(coefs, 'pb')]
    unnamed x40 -> x39, local copies, waits for them, and re-layouts: 12 us -> 9.51 us
  transfers between devices with their start and end apart: 6 -> 6, of which waited for: 5 -> 5; matrix products, arithmetic and copies ran while one was open for 8% -> 9% of each run, Pallas kernels for 0% -> 0%
where the time goes in v1:
time: 509 us; the launch traced here: 500 us
  waiting for transfers between devices  192 us (38%)
  matrix products  141 us (28%)
  other arithmetic  82.5 us (16%)
  local copies, waits for them, and re-layouts  45.8 us (9%)
  starting transfers between devices  23.8 us (5%)
  between operations  15.1 us (3%)
    reduce_scatter x1, waiting for transfers between devices, shards(): lax.psum_scatter(jnp.where(low_rows.T[:, :, None], row_sums[:, :, :column...  78.7 us
    dot_general x1, matrix products, shards(): jnp.einsum('sjhpc,pshi->jci', spectral, fourier_table, precision=HIGHEST)  73.6 us
    all_gather x1, waiting for transfers between devices, shards(): parts = lax.all_gather(coefs, 'pb')  68.5 us
    mul x1, other arithmetic, order_tables(): jnp.cos(angles) * factor  37.4 us
    all_to_all x1, waiting for transfers between devices, shards(): lax.all_to_all(fourier, 'ma', split_axis=0, concat_axis=1, tiled=True)  28.2 us
    dot_general x1, matrix products, shards(): jnp.einsum('srl,src->slc', table_rows, masked, precision=HIGHEST)  26.4 us
    dot_general x1, matrix products, shards(): jnp.einsum('srl,slc->rsc', table_rows, weighted, precision=HIGHEST)  21.9 us
    dot_general x1, matrix products, shards(): jnp.einsum('jci,pshi->sjhpc', rate_of_change_field, fourier_table, precis...  17.4 us
  transfers between devices with their start and end apart: 6, of which 5 were waited for; matrix products, arithmetic and copies ran while one was open for 9% of the time, Pallas kernels for 0%

profile of v1, /device:TPU:1, one launch (start us, length us, event | category | flops | bytes accessed | tf_op | source)
XLA Modules:
  0.0 499.8 jit_solution(7767941320369879879)
XLA Ops:
  9.8 68.5 %all-gather.3.cloned.1.call-done = f32[64,264,64]{1,2,0:T(8,128)} async-done(((f32[16,264,64]{1,2,0:T(8,128)}), f32[64,264,64]{1,2,0:T(8,128)}) %all-gather.3.cloned.1.call-update) | async-done | bytes 4325392 | tf_op jit(solution)/shard_map/all_gather | solution.py:92
  78.3 8.8 %copy.83 = f32[4,16,264,64]{3,2,0,1:T(8,128)} copy(f32[4,16,264,64]{2,3,1,0:T(8,128)} %bitcast.86) | data formatting | bytes 8650752 | tf_op jit(solution)/shard_map/all_gather | solution.py:92
  87.1 10.0 %bitcast_select_fusion.1 = (f32[16,1056,64]{2,1,0:T(8,128)}, f32[16,1056,64]{2,1,0:T(8,128)}) fusion(f32[4,16,264,64]{3,2,0,1:T(8,128)} %copy.83, pred[16,1056]{1,0:T(8,128)(4,1)S(1)} %get-tuple-element.42, pred[16,1056]{1,0:T(8,128)(4,1)S(1)} %get-tuple-element.43), kind=kLoop, calls=%fused_computation.19 | loop fusion | flops 2162688 | bytes 13009920 | tf_op jit(solution)/shard_map/jit(_where)/select_n | solution.py:98
  97.1 26.4 %fusion.60 = f32[16,256,128]{1,2,0:T(8,128)S(1)} fusion(f32[16,1056,1,256]{3,2,1,0:T(1,128)} %param.7, f32[16,1056,64]{2,1,0:T(8,128)} %get-tuple-element.19, f32[16,1056,64]{2,1,0:T(8,128)} %get-tuple-element.18), kind=kOutput, calls=%fused_computation.87 | convolution fusion | flops 6645940224 | bytes 28049408 | tf_op jit(solution)/shard_map/srl,src->slc/dot_general | solution.py:104
  123.6 2.0 copy.84
  125.5 8.3 %all-to-all-start = ((f32[16,256,128]{2,0,1:T(8,128)}), f32[16,256,128]{2,0,1:T(8,128)}, u32[]{:S(2)}, u32[]{:S(2)}) async-start(f32[16,256,128]{2,0,1:T(8,128)} %copy.84), calls=%async_computation | async-start | bytes 4194304 | tf_op jit(solution)/shard_map/all_to_all | solution.py:105
  134.0 2.3 copy.89
  136.4 37.4 %cosine_multiply_fusion = (f32[1,512,2,2048]{3,1,0,2:T(8,128)}, f32[1,512,2,2048]{3,1,0,2:T(8,128)}) fusion(s32[512,2]{0,1:T(2,128)S(1)} %pad_add_fusion), kind=kLoop, calls=%fused_computation.26 | loop fusion | flops 35651584 | bytes 16781312 | tf_op jit(solution)/shard_map/mul | solution.py:48
  173.7 3.8 copy.86
  177.6 10.0 %reshape.241 = f32[512,8,2,2,32]{4,3,2,1,0:T(2,128)} reshape(f32[32,16,8,128]{3,2,1,0:T(8,128)} %copy.86) | data formatting | bytes 4194304 | tf_op jit(solution)/shard_map/reshape | solution.py:109
  187.5 5.6 %broadcast_multiply_fusion = f32[512,8,2,2,32]{4,3,2,1,0:T(2,128)S(1)} fusion(f32[512,8,2,2,32]{4,3,2,1,0:T(2,128)} %reshape.241, f32[512,2]{1,0:T(8,128)S(1)} %copy.87), kind=kLoop, calls=%fused_computation.31 | loop fusion | flops 524288 | bytes 4198400 | tf_op jit(solution)/shard_map/mul | solution.py:109
  193.2 73.6 %fusion.33 = f32[8,32,2048]{2,1,0:T(8,128)S(1)} fusion(f32[512,8,2,2,32]{4,3,2,1,0:T(2,128)S(1)} %broadcast_multiply_fusion, f32[1,512,2,2048]{3,1,0,2:T(8,128)} %get-tuple-element.39, f32[1,512,2,2048]{3,1,0,2:T(8,128)} %get-tuple-element.38), kind=kOutput, calls=%fused_computation.53 | convolution fusion | flops 12889096192 | bytes 20971520 | tf_op jit(solution)/shard_map/sjhpc,pshi->jci/dot_general | solution.py:111
  268.6 2.8 collective-permute-start
  271.4 4.0 collective-permute-start.1
  276.6 14.4 %collective-permute-done = f32[14,2,3,2048]{3,0,2,1:T(8,128)S(1)} collective-permute-done((f32[14,2,3,2048]{3,0,2,1:T(8,128)}, f32[14,2,3,2048]{3,0,2,1:T(8,128)S(1)}, u32[]{:S(2)}, u32[]{:S(2)}) %collective-permute-start) | collective-permute-done | bytes 688160 | tf_op jit(solution)/shard_map/ppermute | solution.py:30
  292.1 1.8 pad_maximum_fusion.9
  297.5 1.6 pad_maximum_fusion
  300.0 2.4 fusion.30
  304.0 1.5 fusion.27
  308.9 1.6 fusion.40
  314.0 2.2 fusion.48
  316.2 1.6 fusion.80
  318.4 17.4 %fusion.57 = f32[512,8,2,2,32]{0,4,1,2,3:T(8,128)S(1)} fusion(f32[8,8,2048]{2,1,0:T(8,128)S(1)} %get-tuple-element.25, f32[8,8,2048]{2,1,0:T(8,128)S(1)} %get-tuple-element.26, f32[8,8,2048]{2,1,0:T(8,128)S(1)} %get-tuple-element.27, f32[8,8,2048]{2,1,0:T(8,128)S(1)} %get-tuple-element.24, f32[1,512,2,2048]{3,1,0,2:T(8,128)} %get-tuple-element.39, ...), kind=kOutput, calls=%fused_computation.86 | convolution fusion | flops 12890669056 | bytes 20971520 | tf_op jit(solution)/shard_map/jci,pshi->sjhpc/dot_general | solution.py:151
  335.7 1.6 copy.109
  337.3 2.9 copy.110
  340.3 8.7 %all-to-all-start.1 = ((f32[512,8,128]{2,1,0:T(8,128)}), f32[512,8,128]{2,1,0:T(8,128)}, u32[]{:S(2)}, u32[]{:S(2)}) async-start(f32[512,8,128]{2,1,0:T(8,128)} %copy.110), calls=%async_computation.1 | async-start | bytes 4194304 | tf_op jit(solution)/shard_map/all_to_all | solution.py:154
  349.1 28.2 %all-to-all-done.1 = f32[512,8,128]{2,1,0:T(8,128)} async-done(((f32[512,8,128]{2,1,0:T(8,128)}), f32[512,8,128]{2,1,0:T(8,128)}, u32[]{:S(2)}, u32[]{:S(2)}) %all-to-all-start.1) | async-done | bytes 2097184 | tf_op jit(solution)/shard_map/all_to_all | solution.py:154
  377.3 21.9 %fusion.20 = f32[1056,16,128]{2,0,1:T(8,128)S(1)} fusion(f32[16,1056,1,256]{3,2,1,0:T(1,128)} %param.7, f32[16,32,8,128]{3,2,0,1:T(8,128)} %bitcast.30, f32[256]{0:T(256)S(1)} %bitcast.93), kind=kOutput, calls=%fused_computation.30 | convolution fusion | flops 6644301824 | bytes 28050432 | tf_op jit(solution)/shard_map/srl,slc->rsc/dot_general | solution.py:157
  399.2 9.5 %fusion.8 = f32[1056,16,64]{2,0,1:T(8,128)} fusion(f32[1056,16,128]{2,0,1:T(8,128)S(1)} %fusion.20, pred[1056,16]{0,1:T(8,128)(4,1)S(1)} %get-tuple-element.41, pred[1056,16]{0,1:T(8,128)(4,1)S(1)} %get-tuple-element.40), kind=kLoop, calls=%fused_computation.13 | loop fusion | flops 3244032 | bytes 13009920 | tf_op jit(solution)/shard_map/add | solution.py:160
  408.7 2.1 copy.113
  410.8 78.7 %reduce-scatter.2.cloned.1.call-done = f32[264,16,64]{2,0,1:T(8,128)} async-done(((f32[1056,16,64]{2,0,1:T(8,128)}), f32[264,16,64]{2,0,1:T(8,128)}) %reduce-scatter.2.cloned.1.call-update) | async-done | bytes 1081360 | tf_op jit(solution)/shard_map/reduce_scatter | solution.py:159
  489.5 3.0 copy.112
  (99 shorter events, 20.0 us)
Async XLA Ops:
  7.2 309.0 %copy-start = (f32[12,2]{0,1:T(2,128)S(1)}, f32[12,2]{0,1:T(2,128)}, u32[]{:S(2)}) copy-start(f32[12,2]{0,1:T(2,128)} %param.11) | copy-start | bytes 292
  7.2 71.1 %all-gather.3.cloned.1.call-start = ((), (), s32[]{:S(2)}) async-start(), calls=%async_computation.4 | async-start | bytes 7864320 | tf_op jit(solution)/shard_map/all_gather | solution.py:92
  8.7 0.5 copy-start.10
  9.2 0.6 copy-start.7
  125.5 8.3 %copy-start.9 = (s32[512]{0:T(512)S(1)}, s32[512]{0:T(512)}, u32[]{:S(2)}) copy-start(s32[512]{0:T(512)} %param.9) | copy-start | bytes 6148
  125.5 48.2 %all-to-all-start = ((f32[16,256,128]{2,0,1:T(8,128)}), f32[16,256,128]{2,0,1:T(8,128)}, u32[]{:S(2)}, u32[]{:S(2)}) async-start(f32[16,256,128]{2,0,1:T(8,128)} %copy.84), calls=%async_computation | async-start | bytes 4194304 | tf_op jit(solution)/shard_map/all_to_all | solution.py:105
  266.8 1.8 copy-start.2
  268.6 22.4 %collective-permute-start = (f32[14,2,3,2048]{3,0,2,1:T(8,128)}, f32[14,2,3,2048]{3,0,2,1:T(8,128)S(1)}, u32[]{:S(2)}, u32[]{:S(2)}) collective-permute-start(f32[14,2,3,2048]{3,0,2,1:T(8,128)} %get-tuple-element.22), channel_id=1, source_target_pairs={{0,1},{1,2},{2,3},{3,4},{4,5},{5,6},{6,7},{7,8},{8,9},{9,10},{10,1... | collective-permute-start | bytes 2064392 | tf_op jit(solution)/shard_map/ppermute | solution.py:30
  271.4 20.7 %collective-permute-start.1 = (f32[14,2,3,2048]{3,0,2,1:T(8,128)}, f32[14,2,3,2048]{3,0,2,1:T(8,128)}, u32[]{:S(2)}, u32[]{:S(2)}) collective-permute-start(f32[14,2,3,2048]{3,0,2,1:T(8,128)} %get-tuple-element.23), channel_id=1, source_target_pairs={{1,0},{2,1},{3,2},{4,3},{5,4},{6,5},{7,6},{8,7},{9,8},{10,9},{11,1... | collective-permute-start | bytes 2064392 | tf_op jit(solution)/shard_map/ppermute | solution.py:31
  307.0 1.2 copy-start.14
  310.5 0.9 copy-start.4
  310.6 1.0 copy-start.6
  310.6 1.0 copy-start.5
  311.7 0.9 copy-start.13
  312.6 1.4 copy-start.1
  313.2 5.1 %slice-start = ((s8[8388608]{0:T(1024)(128)(4,1)}), s8[4194304]{0:T(1024)(128)(4,1)S(1)}, s32[]{:S(2)}) async-start(s8[8388608]{0:T(1024)(128)(4,1)} %bitcast.83), calls=%async_computation.5 | async-start | bytes 8388608
  314.0 4.3 slice-start.1
  316.2 1.8 copy-start.3
  340.3 8.8 %copy-start.8 = (pred[1056]{0:T(1024)(128)(4,1)S(1)}, pred[1056]{0:T(1024)(128)(4,1)}, u32[]{:S(2)}) copy-start(pred[1056]{0:T(1024)(128)(4,1)} %copy-done.7) | copy-start | bytes 3172
  340.3 8.8 %copy-start.11 = (s32[16]{0:T(128)S(1)}, s32[16]{0:T(128)}, u32[]{:S(2)}) copy-start(s32[16]{0:T(128)} %copy-done.10) | copy-start | bytes 196
  340.3 37.1 %copy-start.12 = (f32[1,256]{1,0:T(1,128)S(1)}, f32[1,256]{1,0:T(1,128)}, u32[]{:S(2)}) copy-start(f32[1,256]{1,0:T(1,128)} %param.8) | copy-start | bytes 3076
  340.3 37.1 %all-to-all-start.1 = ((f32[512,8,128]{2,1,0:T(8,128)}), f32[512,8,128]{2,1,0:T(8,128)}, u32[]{:S(2)}, u32[]{:S(2)}) async-start(f32[512,8,128]{2,1,0:T(8,128)} %copy.110), calls=%async_computation.1 | async-start | bytes 4194304 | tf_op jit(solution)/shard_map/all_to_all | solution.py:154
  349.0 140.5 %reduce-scatter.2.cloned.1.call-start = ((), (), s32[]{:S(2)}) async-start(), calls=%async_computation.3 | async-start | bytes 10813440 | tf_op jit(solution)/shard_map/reduce_scatter | solution.py:159
Sparse Core Ops, SparseCore 0:
  9.7 68.6 all-gather.2
  408.9 80.5 reduce-scatter.1
